TPU v7x, 16 devices: a 4x2x1 block of a 4x4x8 slice. The times are simulated.
16 devices in a mesh: rep: 4 (over y, z, core), dp: 4 (over x).
Axes of the slice: x: 4, y: 2, z: 1, core: 2. Of those that a mesh axis runs over, the one named last changes fastest.
The devices are a block of a 4x4x8 slice.
Arguments:
- x: bfloat16 [16, 4096, 768], P(('rep', 'dp')), parts along dimension 0
- dy: bfloat16 [16, 4096, 768], P(('rep', 'dp')), parts along dimension 0
- w_gate: bfloat16 [2, 768, 1792], P(None, 'dp')
- w_up: bfloat16 [2, 768, 1792], P(None, 'dp')
- w_down: bfloat16 [2, 1792, 768], P(None, 'dp')
- m_w_gate: float32 [2, 768, 1792], P(None, 'dp')
- m_w_up: float32 [2, 768, 1792], P(None, 'dp')
- m_w_down: float32 [2, 1792, 768], P(None, 'dp')
- v_w_gate: float32 [2, 768, 1792], P(None, 'dp')
- v_w_up: float32 [2, 768, 1792], P(None, 'dp')
- v_w_down: float32 [2, 1792, 768], P(None, 'dp')
Outputs:
- output 1: bfloat16 [8, 768, 1792], P('rep', 'dp'), parts along dimension 0
- output 2: bfloat16 [8, 768, 1792], P('rep', 'dp'), parts along dimension 0
- output 3: bfloat16 [8, 1792, 768], P('rep', 'dp'), parts along dimension 0
- output 4: float32 [8, 768, 1792], P('rep', 'dp'), parts along dimension 0
- output 5: float32 [8, 768, 1792], P('rep', 'dp'), parts along dimension 0
- output 6: float32 [8, 1792, 768], P('rep', 'dp'), parts along dimension 0
- output 7: float32 [8, 768, 1792], P('rep', 'dp'), parts along dimension 0
- output 8: float32 [8, 768, 1792], P('rep', 'dp'), parts along dimension 0
- output 9: float32 [8, 1792, 768], P('rep', 'dp'), parts along dimension 0
There are 4 independent parts. A program takes and returns all parts, laid end to end along the dimension named above; an argument that names none is the same for every part.
All inputs are finite; a program needn't handle non-finite values.
Results may differ from a plain program's by a relative error of at most 0.022.
Values are sent between devices in bfloat16 or wider.
A program may use at most 768 MiB of HBM per device.

v0:
```python
import jax
import jax.numpy as jnp
from jax import lax
from jax.sharding import PartitionSpec as P

NAMES = ("w_gate", "w_up", "w_down")


def matmul(a, w):
    return jnp.dot(a, w, preferred_element_type=jnp.float32).astype(jnp.bfloat16)


def normed(h):
    wide = h.astype(jnp.float32)
    scale = lax.rsqrt(jnp.mean(wide**2, -1, keepdims=True) + 1e-6)
    return (wide * scale).astype(jnp.bfloat16)


def layer(h, w):
    a = normed(h)
    gate = jnp.dot(a, w["w_gate"], preferred_element_type=jnp.float32)
    up = jnp.dot(a, w["w_up"], preferred_element_type=jnp.float32)
    return h + matmul((jax.nn.silu(gate) * up).astype(jnp.bfloat16), w["w_down"])


def adamw(w, m, v, g):
    m = 0.9 * m + 0.1 * g
    v = 0.95 * v + 0.05 * g * g
    step = m * lax.rsqrt(v + 1e-8) + 0.1 * w
    return (w - 0.02 * step).astype(jnp.bfloat16), m, v


def clipped(gradients, sum_of_squares, count):
    factor = jnp.minimum(1.0, 0.5 * lax.rsqrt(sum_of_squares / count + 1e-30))
    return [g * factor for g in gradients]


def solution(mesh):
    def fetched(weights, number):
        return {name: lax.all_gather(w[number], "dp", axis=0, tiled=True) for name, w in zip(NAMES, weights, strict=True)}

    def step(x, dy, *arrays):
        weights, m, v = (arrays[i : i + 3] for i in (0, 3, 6))
        layers = weights[0].shape[0]
        h, kept = x[0], []
        for number in range(layers):
            kept.append(h)
            h = layer(h, fetched(weights, number))
        by_h, mine = dy[0], [None] * layers
        for number in reversed(range(layers)):
            _, back = jax.vjp(lambda w, h: layer(h, w), fetched(weights, number), kept[number])
            by_w, by_h = back(by_h)
            mine[number] = [lax.psum_scatter(by_w[name], "dp", scatter_dimension=0, tiled=True) for name in NAMES]
        gradients = [jnp.stack([mine[number][i] for number in range(layers)]).astype(jnp.float32) for i in range(3)]
        squares = lax.psum(sum(jnp.sum(g * g) for g in gradients), "dp")
        gradients = clipped(gradients, squares, lax.psum(1, "dp") * sum(g.size for g in gradients))
        new = [adamw(w.astype(jnp.float32), m, v, g) for w, m, v, g in zip(weights, m, v, gradients, strict=True)]
        return tuple(one[which] for which in range(3) for one in new)

    states, cut = P(("rep", "dp"), None, None), P(None, "dp", None)
    return jax.shard_map(
        step,
        mesh=mesh,
        in_specs=(states, states) + (cut,) * 9,
        out_specs=(P("rep", "dp", None),) * 9,
        check_vma=False,
    )
```

profile of v0, /device:TPU:112, one launch (start us, length us, event | category | flops | bytes accessed | tf_op | source)
XLA Modules:
  0.0 579.9 jit_solution(3515908285354876253)
XLA Ops:
  28.6 8.8 %copy.21 = bf16[1,4096,768]{1,2,0:T(8,128)(2,1)} copy(bf16[1,4096,768]{2,1,0:T(8,128)(2,1)} %param.12) | data formatting | bytes 12582912 | tf_op args[1]
  44.9 19.8 %fusion.39 = f32[4096,1792]{1,0:T(8,128)} fusion(bf16[1,4096,768]{1,2,0:T(8,128)(2,1)} %copy.20, f32[4096]{0:T(1024)S(1)} %add_rsqrt_fusion, bf16[1,768,1792]{2,1,0:T(8,128)(2,1)} %all-gather.13.cloned.1.call-done), kind=kOutput, calls=%fused_computation.55 | convolution fusion | flops 11283726336 | bytes 38420480 | tf_op jit(solution)/shard_map/dot_general | solution.py:21
  64.7 14.4 %all-gather.15.cloned.1.call-done = bf16[1,768,1792]{2,1,0:T(8,128)(2,1)} async-done(((bf16[1,192,1792]{2,1,0:T(8,128)(2,1)}), bf16[1,768,1792]{2,1,0:T(8,128)(2,1)}) %all-gather.15.cloned.1.call-update) | async-done | bytes 2752528 | tf_op jit(solution)/shard_map/all_gather | solution.py:40
  79.1 33.4 %multiply_convert_fusion.1 = (bf16[4096,1792]{1,0:T(8,128)(2,1)}, f32[4096,1792]{1,0:T(8,128)}) fusion(f32[4096,1792]{1,0:T(8,128)} %fusion.39, bf16[1,768,1792]{2,1,0:T(8,128)(2,1)} %all-gather.15.cloned.1.call-done, bf16[1,4096,768]{1,2,0:T(8,128)(2,1)} %copy.20, f32[4096]{0:T(1024)S(1)} %add_rsqrt_fusion), kind=kOutput, calls=%fused_computation.17 | convolution fusion | flops 11327766528 | bytes 82460672 | tf_op jit(solution)/shard_map/dot_general | solution.py:22
  113.3 19.2 %fusion.19 = (f32[4096]{0:T(1024)S(1)}, bf16[4096,768]{0,1:T(8,128)(2,1)}) fusion(bf16[4096,1792]{1,0:T(8,128)(2,1)} %get-tuple-element.24, bf16[1,1792,768]{2,1,0:T(8,128)(2,1)} %all-gather.17.cloned.1.call-done, bf16[1,4096,768]{1,2,0:T(8,128)(2,1)} %copy.20), kind=kOutput, calls=%fused_computation.37 | convolution fusion | flops 11290013696 | bytes 30031872 | tf_op jit(solution)/shard_map/dot_general | solution.py:10
  132.5 14.9 %all-gather.23.cloned.1.call-done = bf16[1,768,1792]{2,1,0:T(8,128)(2,1)} async-done(((bf16[1,192,1792]{2,1,0:T(8,128)(2,1)}), bf16[1,768,1792]{2,1,0:T(8,128)(2,1)}) %all-gather.23.cloned.1.call-update) | async-done | bytes 2752528 | tf_op jit(solution)/shard_map/all_gather | solution.py:40
  147.4 20.2 %fusion.31 = f32[4096,1792]{1,0:T(8,128)} fusion(bf16[4096,768]{0,1:T(8,128)(2,1)} %get-tuple-element.27, f32[4096]{0:T(1024)S(1)} %fusion.88, bf16[1,768,1792]{2,1,0:T(8,128)(2,1)} %all-gather.23.cloned.1.call-done), kind=kOutput, calls=%fused_computation.52 | convolution fusion | flops 11283726336 | bytes 38420480 | tf_op jit(solution)/shard_map/jvp()/dot_general | solution.py:22
  167.5 13.9 %all-gather.21.cloned.1.call-done = bf16[1,1792,768]{2,1,0:T(8,128)(2,1)} async-done(((bf16[1,448,768]{2,1,0:T(8,128)(2,1)}), bf16[1,1792,768]{2,1,0:T(8,128)(2,1)}) %all-gather.21.cloned.1.call-update) | async-done | bytes 2752528 | tf_op jit(solution)/shard_map/all_gather | solution.py:40
  181.4 17.5 %convolution_convert_fusion.1 = bf16[4096,1792]{1,0:T(8,128)(2,1)} fusion(bf16[1,4096,768]{2,1,0:T(8,128)(2,1)} %param.12, bf16[1,1792,768]{2,1,0:T(8,128)(2,1)} %all-gather.21.cloned.1.call-done), kind=kOutput, calls=%fused_computation.30 | convolution fusion | flops 11281629184 | bytes 23724032 | tf_op jit(solution)/shard_map/transpose(jvp())/dot_general | solution.py:10
  199.0 16.5 %all-gather.19.cloned.1.call-done = bf16[1,768,1792]{2,1,0:T(8,128)(2,1)} async-done(((bf16[1,192,1792]{2,1,0:T(8,128)(2,1)}), bf16[1,768,1792]{2,1,0:T(8,128)(2,1)}) %all-gather.19.cloned.1.call-update) | async-done | bytes 2752528 | tf_op jit(solution)/shard_map/all_gather | solution.py:40
  215.5 39.7 %fusion.2 = (bf16[4096,1792]{1,0:T(8,128)(2,1)}, f32[4096,1792]{1,0:T(8,128)}) fusion(f32[4096,1792]{1,0:T(8,128)} %fusion.31, bf16[4096,1792]{1,0:T(8,128)(2,1)} %convolution_convert_fusion.1, bf16[1,768,1792]{2,1,0:T(8,128)(2,1)} %all-gather.19.cloned.1.call-done, bf16[4096,768]{0,1:T(8,128)(2,1)} %get-tuple-element.27, f32[4096]{0:T(1024)S(1)} %fusion.88), kind=kOutput, calls=%fused_computation.8 | convolution fusion | flops 11371806720 | bytes 97140736 | tf_op jit(solution)/shard_map/jvp()/dot_general | solution.py:21
  255.2 18.8 %fusion.49 = bf16[768,1792]{1,0:T(8,128)(2,1)} fusion(bf16[4096,1792]{1,0:T(8,128)(2,1)} %get-tuple-element.28, bf16[4096,768]{0,1:T(8,128)(2,1)} %get-tuple-element.27, f32[4096]{0:T(1024)S(1)} %fusion.88), kind=kOutput, calls=%fused_computation.71 | convolution fusion | flops 11283726336 | bytes 23740416 | tf_op jit(solution)/shard_map/transpose(jvp())/dot_general | solution.py:21
  274.2 23.2 %fusion.22 = bf16[4096,768]{0,1:T(8,128)(2,1)} fusion(bf16[4096,1792]{1,0:T(8,128)(2,1)} %convolution_convert_fusion.1, bf16[1,768,1792]{2,1,0:T(8,128)(2,1)} %all-gather.23.cloned.1.call-done, f32[4096,1792]{1,0:T(8,128)} %get-tuple-element.29), kind=kOutput, calls=%fused_computation.40 | convolution fusion | flops 11321475072 | bytes 53084160 | tf_op jit(solution)/shard_map/transpose(jvp())/dot_general | solution.py:22
  297.4 20.5 %fusion.21 = (f32[4096]{0:T(1024)S(1)}, bf16[4096,768]{0,1:T(8,128)(2,1)}) fusion(bf16[4096,768]{0,1:T(8,128)(2,1)} %get-tuple-element.27, bf16[4096,768]{0,1:T(8,128)(2,1)} %fusion.22, bf16[4096,1792]{1,0:T(8,128)(2,1)} %get-tuple-element.28, bf16[1,768,1792]{2,1,0:T(8,128)(2,1)} %all-gather.19.cloned.1.call-done), kind=kOutput, calls=%fused_computation.39 | convolution fusion | flops 11290013696 | bytes 36323328 | tf_op jit(solution)/shard_map/transpose(jvp())/dot_general | solution.py:21
  318.0 9.7 %fusion.23 = bf16[4096,768]{0,1:T(8,128)(2,1)} fusion(bf16[4096,768]{0,1:T(8,128)(2,1)} %get-tuple-element.27, bf16[4096,768]{0,1:T(8,128)(2,1)} %get-tuple-element.31, bf16[1,4096,768]{1,2,0:T(8,128)(2,1)S(1)} %bitcast.69, f32[4096]{0:T(1024)S(1)} %multiply_multiply_fusion.3, f32[4096]{0:T(1024)S(1)} %fusion.88), kind=kLoop, calls=%fused_computation.43 | loop fusion | flops 22020096 | bytes 25198592 | tf_op jit(solution)/shard_map/transpose(jvp())/add_any | solution.py:14
  327.6 20.0 %convolution_convert_fusion = bf16[4096,1792]{1,0:T(8,128)(2,1)} fusion(bf16[4096,768]{0,1:T(8,128)(2,1)} %fusion.23, bf16[1,1792,768]{2,1,0:T(8,128)(2,1)S(1)} %copy-done.16), kind=kOutput, calls=%fused_computation.29 | convolution fusion | flops 11281629184 | bytes 23724032 | tf_op jit(solution)/shard_map/transpose(jvp())/dot_general | solution.py:10
  347.6 30.0 %fusion.41 = bf16[768,1792]{1,0:T(8,128)(2,1)} fusion(f32[4096,1792]{1,0:T(8,128)} %fusion.39, f32[4096,1792]{1,0:T(8,128)} %get-tuple-element.25, bf16[4096,1792]{1,0:T(8,128)(2,1)} %convolution_convert_fusion, bf16[1,4096,768]{1,2,0:T(8,128)(2,1)} %copy.20, f32[4096]{0:T(1024)S(1)} %copy-done.15), kind=kOutput, calls=%fused_computation.68 | convolution fusion | flops 11365842944 | bytes 82460672 | tf_op jit(solution)/shard_map/transpose(jvp())/dot_general | solution.py:21
  377.7 25.2 %fusion.55 = bf16[768,1792]{1,0:T(8,128)(2,1)} fusion(bf16[4096,1792]{1,0:T(8,128)(2,1)} %convolution_convert_fusion.1, bf16[4096,768]{0,1:T(8,128)(2,1)} %get-tuple-element.27, f32[4096]{0:T(1024)S(1)} %fusion.88, f32[4096,1792]{1,0:T(8,128)} %get-tuple-element.29), kind=kOutput, calls=%fused_computation.73 | convolution fusion | flops 11329142784 | bytes 53100544 | tf_op jit(solution)/shard_map/transpose(jvp())/dot_general | solution.py:22
  403.1 25.4 %fusion.46 = bf16[768,1792]{1,0:T(8,128)(2,1)} fusion(bf16[4096,1792]{1,0:T(8,128)(2,1)} %convolution_convert_fusion, f32[4096,1792]{1,0:T(8,128)} %fusion.39, bf16[1,4096,768]{1,2,0:T(8,128)(2,1)} %copy.20, f32[4096]{0:T(1024)S(1)} %copy-done.15), kind=kOutput, calls=%fused_computation.69 | convolution fusion | flops 11329142784 | bytes 53100544 | tf_op jit(solution)/shard_map/transpose(jvp())/dot_general | solution.py:22
  428.6 26.1 %fusion.52 = bf16[1792,768]{1,0:T(8,128)(2,1)} fusion(bf16[1,4096,768]{2,1,0:T(8,128)(2,1)} %param.12, f32[4096,1792]{1,0:T(8,128)} %fusion.31, f32[4096,1792]{1,0:T(8,128)} %get-tuple-element.29), kind=kOutput, calls=%fused_computation.72 | convolution fusion | flops 11319705600 | bytes 67764224 | tf_op jit(solution)/shard_map/transpose(jvp())/dot_general | solution.py:10
  454.9 17.8 %convolution_convert_fusion.4 = bf16[1792,768]{1,0:T(8,128)(2,1)} fusion(bf16[4096,1792]{1,0:T(8,128)(2,1)} %get-tuple-element.24, bf16[4096,768]{0,1:T(8,128)(2,1)} %fusion.23), kind=kOutput, calls=%fused_computation.70 | convolution fusion | flops 11275665408 | bytes 23724032 | tf_op jit(solution)/shard_map/transpose(jvp())/dot_general | solution.py:10
  480.0 29.7 %reduce-scatter.17.cloned.1.call-done = bf16[448,768]{1,0:T(8,128)(2,1)} async-done(((bf16[1792,768]{1,0:T(8,128)(2,1)}), bf16[448,768]{1,0:T(8,128)(2,1)}) %reduce-scatter.17.cloned.1.call-update) | async-done | bytes 688144 | tf_op jit(solution)/shard_map/reduce_scatter | solution.py:53
  509.7 33.5 %reduce-scatter.15.cloned.1.call-done = bf16[448,768]{1,0:T(8,128)(2,1)} async-done(((bf16[1792,768]{1,0:T(8,128)(2,1)}), bf16[448,768]{1,0:T(8,128)(2,1)}) %reduce-scatter.15.cloned.1.call-update) | async-done | bytes 688144 | tf_op jit(solution)/shard_map/reduce_scatter | solution.py:53
  546.5 9.1 %psum.7 = f32[]{:T(128)} all-reduce(f32[]{:T(128)S(6)} %add.99), channel_id=1, replica_groups=mesh['rep'=4,'dp'=4] {'dp'}, use_global_device_ids=true, to_apply=%region_12.13 | all-reduce | flops 1 | bytes 8 | tf_op jit(solution)/shard_map/psum | solution.py:55
  (82 shorter events, 55.1 us)
Async XLA Ops:
  7.2 37.7 %all-gather.13.cloned.1.call-start = ((), (), s32[]{:S(2)}) async-start(), calls=%async_computation.12 | async-start | bytes 3440640 | tf_op jit(solution)/shard_map/all_gather | solution.py:40
  9.9 69.2 %all-gather.15.cloned.1.call-start = ((), (), s32[]{:S(2)}) async-start(), calls=%async_computation.13 | async-start | bytes 3440640 | tf_op jit(solution)/shard_map/all_gather | solution.py:40
  12.5 100.8 %all-gather.17.cloned.1.call-start = ((), (), s32[]{:S(2)}) async-start(), calls=%async_computation.14 | async-start | bytes 3440640 | tf_op jit(solution)/shard_map/all_gather | solution.py:40
  13.8 133.6 %all-gather.23.cloned.1.call-start = ((), (), s32[]{:S(2)}) async-start(), calls=%async_computation.17 | async-start | bytes 3440640 | tf_op jit(solution)/shard_map/all_gather | solution.py:40
  14.5 167.0 %all-gather.21.cloned.1.call-start = ((), (), s32[]{:S(2)}) async-start(), calls=%async_computation.16 | async-start | bytes 3440640 | tf_op jit(solution)/shard_map/all_gather | solution.py:40
  15.1 200.4 %all-gather.19.cloned.1.call-start = ((), (), s32[]{:S(2)}) async-start(), calls=%async_computation.15 | async-start | bytes 3440640 | tf_op jit(solution)/shard_map/all_gather | solution.py:40
  15.7 457.0 %reduce-scatter.9.cloned.1.call-start = ((), (), s32[]{:S(2)}) async-start(), calls=%async_computation.7 | async-start | bytes 3440640 | tf_op jit(solution)/shard_map/reduce_scatter | solution.py:53
  28.6 50.5 %copy-start.14 = (f32[4096]{0:T(1024)}, f32[4096]{0:T(1024)S(1)}, u32[]{:S(2)}) copy-start(f32[4096]{0:T(1024)S(1)} %add_rsqrt_fusion) | copy-start | bytes 49156
  132.5 35.0 %copy-start.12 = (f32[4096]{0:T(1024)}, f32[4096]{0:T(1024)S(1)}, u32[]{:S(2)}) copy-start(f32[4096]{0:T(1024)S(1)} %get-tuple-element.26) | copy-start | bytes 49156
  255.2 62.7 %slice-start = ((s8[6291456]{0:T(1024)(128)(4,1)}), s8[2097152]{0:T(1024)(128)(4,1)S(1)}, s32[]{:S(2)}) async-start(s8[6291456]{0:T(1024)(128)(4,1)} %bitcast.68), calls=%async_computation.18 | async-start | bytes 4194304
  274.1 198.7 %reduce-scatter.7.cloned.1.call-start = ((), (), s32[]{:S(2)}) async-start(), calls=%async_computation.6 | async-start | bytes 3440640 | tf_op jit(solution)/shard_map/reduce_scatter | solution.py:53
  274.2 43.8 %slice-start.1 = ((s8[6291456]{0:T(1024)(128)(4,1)}), s8[4194304]{0:T(1024)(128)(4,1)S(1)}, s32[]{:S(2)}) async-start(s8[6291456]{0:T(1024)(128)(4,1)} %bitcast.68), calls=%async_computation.19 | async-start | bytes 8388608
  297.4 20.5 %copy-start.13 = (f32[4096]{0:T(1024)S(1)}, f32[4096]{0:T(1024)}, u32[]{:S(2)}) copy-start(f32[4096]{0:T(1024)} %copy-done.12) | copy-start | bytes 49156
  317.9 9.7 %copy-start.16 = (bf16[1,1792,768]{2,1,0:T(8,128)(2,1)S(1)}, bf16[1,1792,768]{2,1,0:T(8,128)(2,1)}, u32[]{:S(2)}) copy-start(bf16[1,1792,768]{2,1,0:T(8,128)(2,1)} %all-gather.17.cloned.1.call-done) | copy-start | bytes 8257540
  327.6 20.0 %copy-start.15 = (f32[4096]{0:T(1024)S(1)}, f32[4096]{0:T(1024)}, u32[]{:S(2)}) copy-start(f32[4096]{0:T(1024)} %copy-done.14) | copy-start | bytes 49156
  377.7 97.8 %reduce-scatter.13.cloned.1.call-start = ((), (), s32[]{:S(2)}) async-start(), calls=%async_computation.9 | async-start | bytes 3440640 | tf_op jit(solution)/shard_map/reduce_scatter | solution.py:53
  403.0 73.1 %reduce-scatter.11.cloned.1.call-start = ((), (), s32[]{:S(2)}) async-start(), calls=%async_computation.8 | async-start | bytes 3440640 | tf_op jit(solution)/shard_map/reduce_scatter | solution.py:53
  428.6 81.1 %reduce-scatter.17.cloned.1.call-start = ((), (), s32[]{:S(2)}) async-start(), calls=%async_computation.11 | async-start | bytes 3440640 | tf_op jit(solution)/shard_map/reduce_scatter | solution.py:53
  454.8 88.3 %reduce-scatter.15.cloned.1.call-start = ((), (), s32[]{:S(2)}) async-start(), calls=%async_computation.10 | async-start | bytes 3440640 | tf_op jit(solution)/shard_map/reduce_scatter | solution.py:53
  472.6 83.7 %copy-start.3 = (bf16[2,448,768]{2,1,0:T(8,128)(2,1)S(1)}, bf16[2,448,768]{2,1,0:T(8,128)(2,1)}, u32[]{:S(2)}) copy-start(bf16[2,448,768]{2,1,0:T(8,128)(2,1)} %param.15) | copy-start | bytes 4128772
  543.1 19.7 %copy-start.10 = (bf16[192,1792]{1,0:T(8,128)(2,1)S(1)}, bf16[192,1792]{1,0:T(8,128)(2,1)}, u32[]{:S(2)}) copy-start(bf16[192,1792]{1,0:T(8,128)(2,1)} %reduce-scatter.13.cloned.1.call-done) | copy-start | bytes 2064388
  543.1 19.7 %copy-start.11 = (bf16[192,1792]{1,0:T(8,128)(2,1)S(1)}, bf16[192,1792]{1,0:T(8,128)(2,1)}, u32[]{:S(2)}) copy-start(bf16[192,1792]{1,0:T(8,128)(2,1)} %reduce-scatter.11.cloned.1.call-done) | copy-start | bytes 2064388
  556.4 9.5 %copy-start.8 = (bf16[192,1792]{1,0:T(8,128)(2,1)S(1)}, bf16[192,1792]{1,0:T(8,128)(2,1)}, u32[]{:S(2)}) copy-start(bf16[192,1792]{1,0:T(8,128)(2,1)} %reduce-scatter.9.cloned.1.call-done) | copy-start | bytes 2064388
  556.4 9.7 %copy-start.9 = (bf16[192,1792]{1,0:T(8,128)(2,1)S(1)}, bf16[192,1792]{1,0:T(8,128)(2,1)}, u32[]{:S(2)}) copy-start(bf16[192,1792]{1,0:T(8,128)(2,1)} %reduce-scatter.7.cloned.1.call-done) | copy-start | bytes 2064388
  (7 other events, 50.7 us)
Sparse Core Ops, SparseCore 0:
  10.2 34.6 all-gather.12
  47.0 32.0 all-gather.14
  81.2 32.0 all-gather.16
  115.3 32.0 all-gather.22
  149.3 32.0 all-gather.20
  183.4 32.0 all-gather.18
  274.2 31.1 reduce-scatter.8
  377.8 31.1 reduce-scatter.6
  411.9 30.6 reduce-scatter.12
  445.3 30.6 reduce-scatter.10
  479.0 30.6 reduce-scatter.16
  512.4 30.6 reduce-scatter.14
where the time goes:
time: 587 us; the launch traced here: 580 us
  matrix products  357 us (61%)
  waiting for transfers between devices  134 us (23%)
  other arithmetic  34.7 us (6%)
  local copies, waits for them, and re-layouts  27.1 us (5%)
  between operations  17.5 us (3%)
  blocking collectives  9.14 us (2%)
    dot_general x5, matrix products, layer(): gate = jnp.dot(a, w['w_gate'], preferred_element_type=jnp.float32)  129 us
    dot_general x5, matrix products, layer(): up = jnp.dot(a, w['w_up'], preferred_element_type=jnp.float32)  127 us
    dot_general x5, matrix products, matmul(): jnp.dot(a, w, preferred_element_type=jnp.float32).astype(jnp.bfloat16)  101 us
    all_gather x6, waiting for transfers between devices, fetched(): lax.all_gather(w[number], 'dp', axis=0, tiled=True)  67.9 us
    reduce_scatter x6, waiting for transfers between devices, step(): lax.psum_scatter(by_w[name], 'dp', scatter_dimension=0, tiled=True)  63.8 us
    unnamed x40, local copies, waits for them, and re-layouts  20.9 us
    convert_element_type x2, other arithmetic, adamw(): return ((w - 0.02 * step).astype(jnp.bfloat16), m, v)  12.9 us
  transfers between devices with their start and end apart: 12, of which 9 were waited for; matrix products, arithmetic and copies ran while one was open for 58% of the time, Pallas kernels for 0%

commit v1 on v0

v1 whole, which is shorter than its diff:
```python
import functools

import jax
import jax.numpy as jnp
from jax import lax
from jax.experimental import pallas as pl
from jax.experimental.pallas import tpu as pltpu
from jax.sharding import PartitionSpec as P

MESH = pl.DeviceIdType.MESH
F32, BF16 = jnp.float32, jnp.bfloat16
ANY = pl.BlockSpec(memory_space=pl.ANY)
IN_VMEM = pl.BlockSpec(memory_space=pltpu.VMEM)
DMA = pltpu.SemaphoreType.DMA
MIB = 2**20
WIDTH = 64


def dot(a, b, ca=1, cb=0):
    return lax.dot_general(a, b, (((ca,), (cb,)), ((), ())), preferred_element_type=F32)


def rows(index, size):
    return pl.ds(pl.multiple_of(index * size, size), size)


def at(start, size):
    return pl.ds(pl.multiple_of(start, 16), size)


def normed(h):
    wide = h.astype(F32)
    scale = lax.rsqrt(jnp.mean(wide * wide, -1, keepdims=True) + 1e-6)
    return (wide * scale).astype(BF16)


def around(n):
    me = lax.axis_index("dp")
    return me, lax.rem(me + n - 1, n), lax.rem(me + 1, n), lax.rem(me + 2, n)


def meet(where):
    barrier = pltpu.get_barrier_semaphore()
    for device in where:
        pl.semaphore_signal(barrier, inc=1, device_id=device, device_id_type=MESH)
    pl.semaphore_wait(barrier, len(where))


def remote(source, target, send, receive, device):
    return pltpu.make_async_remote_copy(
        src_ref=source, dst_ref=target, send_sem=send, recv_sem=receive, device_id=device, device_id_type=MESH
    )


KINDS = 18


def forward_kernel(
    n, x_h, dy_h, wg, wu, wd, gu_o, d_o, a_o, at_o, dyt_o, h_o, a1_o, a1t_o,
    xv, av, dyv, acts, gw, dw, packed, tst, tst2, hst, ast, ssem, rsem, xsem, dysem, osem, wsem,
):
    layers, chunks = gw.shape[0], gw.shape[1]
    tokens, dim = xv.shape
    own, hidden = wg.shape[1], dw.shape[2]
    share, third = wd.shape[1] // chunks, own // 4
    steps = layers * chunks
    tile = dyv.shape[1]
    tiles = tokens // tile
    me, left, right, across = around(n)
    rep = lax.axis_index("rep")
    core, side = lax.rem(rep, 2), lax.rem(rep // 2, 2)
    mate, twin = rep + 1 - 2 * core, rep + 2 - 4 * side

    def x_in(t):
        return pltpu.make_async_copy(x_h.at[rows(t, tile)], xv.at[rows(t, tile)], xsem.at[t])

    def dy_in(t):
        return pltpu.make_async_copy(dy_h.at[rows(t, tile)], dyv.at[lax.rem(t, 2)], dysem.at[lax.rem(t, 2)])

    def start_x(t, _):
        x_in(t).start()
        return 0

    lax.fori_loop(0, tiles, start_x, 0)
    dy_in(0).start()
    dy_in(1).start()

    for layer in range(layers):
        gate, up = wg[layer], wu[layer]
        for j in range(chunks):
            pieces = [w[:, o * share * chunks + j * share : o * share * chunks + (j + 1) * share] for w in (gate, up) for o in range(n)]
            packed[layer * chunks + j] = jnp.concatenate(pieces, -1)

    def place(s, _):
        layer, j = s // chunks, lax.rem(s, chunks)
        gw[layer, j, at(me * own, own), :] = packed[s]
        dw[layer, j, at(me * share, share), :] = wd[layer, rows(j, share), :]
        return 0

    lax.fori_loop(0, steps, place, 0)

    meet([{"dp": left}, {"dp": right}, {"rep": mate}, {"rep": twin}])

    def up_part(s, owner, which):
        return gw.at[s // chunks, lax.rem(s, chunks), at(owner * own + which * 2 * third + core * third, third), :]

    def down_part(s, owner):
        return dw.at[s // chunks, lax.rem(s, chunks), at(owner * share + core * (share // 2), share // 2), :]

    others = (left, right, across)

    def copy(s, kind):
        if kind < 4:
            ref = down_part(s, me) if kind % 2 else up_part(s, me, side)
            device = {"dp": right if kind < 2 else left}
        elif kind == 4:
            ref, device = up_part(s, left, side), {"dp": right}
        elif kind == 5:
            ref, device = down_part(s, right), {"dp": left}
        elif kind < 9:
            ref, device = up_part(s, others[kind - 6], side), {"rep": twin}
        elif kind < 15:
            owner = others[(kind - 9) // 2]
            ref, device = (up_part(s, owner, side) if kind % 2 else down_part(s, owner)), {"rep": mate}
        else:
            ref, device = up_part(s, others[kind - 15], 1 - side), {"rep": mate}
        return remote(ref, ref, ssem.at[s, kind], rsem.at[s, kind], device)

    def weights_out(s):
        layer, j = s // chunks, lax.rem(s, chunks)
        return (
            pltpu.make_async_copy(gw.at[layer, j], gu_o.at[layer, j], wsem.at[s, 0]),
            pltpu.make_async_copy(dw.at[layer, j], d_o.at[layer, j], wsem.at[s, 1]),
        )

    def stage(s, wait, begin):
        @pl.when((s >= 0) & (s < steps))
        def _():
            for kind in wait:
                copy(s, kind).wait_recv()
            for kind in begin:
                copy(s, kind).start()

    def tick(k):
        stage(k + 1, (), (0, 1, 2, 3))
        stage(k - 1, (0, 1, 2, 3), (4, 5, 6, 7, 9, 10, 11, 12))
        stage(k - 2, (4, 5), (8, 13, 14))
        stage(k - 3, (6, 7, 8), (15, 16, 17))
        stage(k - 4, range(9, KINDS), ())

        @pl.when((k >= 4) & (k - 4 < steps))
        def _():
            for c in weights_out(k - 4):
                c.start()

    def at_out(t, slot):
        return pltpu.make_async_copy(tst.at[slot], at_o.at[:, rows(t, tile)], osem.at[slot, 0])

    def dyt_out(t, slot):
        return pltpu.make_async_copy(tst2.at[slot], dyt_o.at[:, rows(t, tile)], osem.at[slot, 1])

    def prepare(t, slot):
        x_in(t).wait()
        dy_in(t).wait()

        @pl.when(t >= 2)
        def _():
            at_out(t, slot).wait()
            dyt_out(t, slot).wait()

        a = normed(xv[rows(t, tile), :])
        av[rows(t, tile), :] = a
        tst[slot] = a.T
        tst2[slot] = dyv[slot].T
        at_out(t, slot).start()
        dyt_out(t, slot).start()

        @pl.when(t + 2 < tiles)
        def _():
            dy_in(t + 2).start()

    stage(0, (), (0, 1, 2, 3))

    def open_(k, _):
        tick(k)
        prepare(2 * k, 0)
        prepare(2 * k + 1, 1)
        return 0

    lax.fori_loop(0, 4, open_, 0)
    tick(4)
    a_out = pltpu.make_async_copy(av, a_o, osem.at[0, 2])
    a_out.start()
    big = 2 * tile

    def chunk(j, _):
        def part(t, _):
            gu = dot(av[rows(t, big), :], gw[0, j])
            gate, up = gu[:, :hidden], gu[:, hidden:]
            acts[rows(t, big), rows(j, hidden)] = (gate * jax.nn.sigmoid(gate) * up).astype(BF16)
            return 0

        lax.fori_loop(0, tokens // big, part, 0)
        tick(j + 5)
        return 0

    lax.fori_loop(0, chunks, chunk, 0)
    for slot in range(2):
        at_out(0, slot).wait()
        dyt_out(0, slot).wait()

    def outs(t):
        slot = lax.rem(t, 2)
        return (
            pltpu.make_async_copy(hst.at[slot], h_o.at[rows(t, tile)], osem.at[slot, 3]),
            pltpu.make_async_copy(ast.at[slot], a1_o.at[rows(t, tile)], osem.at[slot, 4]),
            pltpu.make_async_copy(tst.at[slot], a1t_o.at[:, rows(t, tile)], osem.at[slot, 5]),
        )

    def close(t, _):
        slot = lax.rem(t, 2)

        @pl.when(t >= 2)
        def _():
            for c in outs(t):
                c.wait()

        y = dot(acts[rows(t, tile), :], dw[0].reshape(chunks * hidden, dim)).astype(BF16)
        h = (xv[rows(t, tile), :].astype(F32) + y.astype(F32)).astype(BF16)
        a = normed(h)
        hst[slot] = h
        ast[slot] = a
        tst[slot] = a.T
        for c in outs(t):
            c.start()
        tick(chunks + 5 + t)
        return 0

    lax.fori_loop(0, tiles, close, 0)
    for t in (tiles - 2, tiles - 1):
        for c in outs(t):
            c.wait()
    a_out.wait()

    def finish(s, _):
        for kind in range(KINDS):
            copy(s, kind).wait_send()
        for c in weights_out(s):
            c.wait()
        return 0

    lax.fori_loop(0, steps, finish, 0)


def forward(n, x, dy, wg, wu, wd):
    tokens, dim = x.shape
    layers, own, units = wg.shape
    chunks = wd.shape[1] // WIDTH
    hidden = n * WIDTH
    tile = 512
    V = pltpu.VMEM
    S = jax.ShapeDtypeStruct
    return pl.pallas_call(
        functools.partial(forward_kernel, n),
        out_shape=[
            S((layers, chunks, dim, 2 * hidden), BF16), S((layers, chunks, hidden, dim), BF16),
            S((tokens, dim), BF16), S((dim, tokens), BF16), S((dim, tokens), BF16),
            S((tokens, dim), BF16), S((tokens, dim), BF16), S((dim, tokens), BF16),
        ],
        in_specs=[ANY, ANY, IN_VMEM, IN_VMEM, IN_VMEM],
        out_specs=[ANY] * 8,
        scratch_shapes=[
            V((tokens, dim), BF16), V((tokens, dim), BF16), V((2, tile, dim), BF16), V((tokens, units), BF16),
            V((layers, chunks, dim, 2 * hidden), BF16), V((layers, chunks, hidden, dim), BF16),
            V((layers * chunks, own, 2 * hidden), BF16), V((2, dim, tile), BF16), V((2, dim, tile), BF16), V((2, tile, dim), BF16), V((2, tile, dim), BF16),
            DMA((layers * chunks, KINDS)), DMA((layers * chunks, KINDS)),
            DMA((tokens // tile,)), DMA((2,)), DMA((2, 6)), DMA((layers * chunks, 2)),
        ],
        compiler_params=pltpu.CompilerParams(collective_id=0, has_side_effects=True, vmem_limit_bytes=63 * MIB),
        name="forward",
    )(x, dy, wg, wu, wd)


def backward_kernel(n, deep, *refs):
    it = iter(refs)
    take = lambda count: [next(it) for _ in range(count)]
    a_h, at_h, dy_h, dyt_h, gu_all, d_all, extra = take(7)
    gu_h, d_h = gu_all.at[1 if deep else 0], d_all.at[1 if deep else 0]
    og, od, sq = take(3)
    if deep:
        dgu_o, dx_o, dxt_o = take(3)
    av, atv, dyv, dytv, dgu, act, gw, dw, tg, td, rg, rd, sqg, sqd, ssem, rsem, isem, wsem = take(18)
    if deep:
        flat, wide, hst, xtst, dsem, fsem, psem, osem = take(8)
    else:
        tot, csem = take(2)
    tokens, dim = av.shape
    chunks, hidden = d_all.shape[1:3]
    own, share = dim // n, hidden // n
    g2, d2 = own // 2, share // 2
    big = 1024
    parts = tokens // big
    me, left, right, across = around(n)

    def a_in(t):
        return pltpu.make_async_copy(a_h.at[rows(t, big)], av.at[rows(t, big)], isem.at[0, t])

    def dy_in(t):
        return pltpu.make_async_copy(dy_h.at[rows(t, big)], dyv.at[rows(t, big)], isem.at[1, t])

    late = (pltpu.make_async_copy(at_h, atv, isem.at[2, 0]), pltpu.make_async_copy(dyt_h, dytv, isem.at[2, 1]))

    def w_in(j):
        s = lax.rem(j, 2)
        return (pltpu.make_async_copy(gu_h.at[j], gw.at[s], wsem.at[s, 0]), pltpu.make_async_copy(d_h.at[j], dw.at[s], wsem.at[s, 1]))

    for c in w_in(0):
        c.start()
    for t in range(parts):
        a_in(t).start()
        dy_in(t).start()
    for c in late:
        c.start()
    sqg[...] = jnp.zeros_like(sqg)
    sqd[...] = jnp.zeros_like(sqd)
    meet([{"dp": left}, {"dp": right}] + ([] if deep else [{"dp": across}]))

    def copy(j, unit, matrix):
        slot = lax.rem(j, 3)
        term, half, block = (tg, g2, own) if matrix == 0 else (td, d2, share)
        device = {"dp": right if unit % 2 == 0 else left}
        if unit < 2:
            source = term.at[slot, at(across * block + unit * half, half), :]
        elif unit < 4:
            owner, which = (right, 1) if unit == 2 else (left, 0)
            source = term.at[slot, at(owner * block + which * half, half), :]
        else:
            owner, which = (right, 0) if unit == 4 else (left, 1)
            source = term.at[slot, at(owner * block + which * half, half), :]
        target = (rg if matrix == 0 else rd).at[j, unit]
        return remote(source, target, ssem.at[j, 2 * unit + matrix], rsem.at[j, 2 * unit + matrix], device)

    def send_terms(j):
        for unit in (0, 1, 2, 3):
            for matrix in (0, 1):
                copy(j, unit, matrix).start()

    def pass_on(j):
        slot = lax.rem(j, 3)
        for unit in (0, 1):
            owner = right if unit == 0 else left
            for matrix, (term, half, block, got) in enumerate(((tg, g2, own, rg), (td, d2, share, rd))):
                copy(j, unit, matrix).wait_recv()
                place = at(owner * block + unit * half, half)
                term[slot, place, :] = (term[slot, place, :].astype(F32) + got[j, unit].astype(F32)).astype(BF16)
                copy(j, unit + 4, matrix).start()

    def settle(j):
        slot = lax.rem(j, 3)
        for unit in (2, 3, 4, 5):
            for matrix in (0, 1):
                copy(j, unit, matrix).wait_recv()
        for matrix, (term, half, block, got, out, total) in enumerate(((tg, g2, own, rg, og, sqg), (td, d2, share, rd, od, sqd))):
            for which in (0, 1):
                mine = term[slot, at(me * block + which * half, half), :].astype(F32)
                single, summed = (3, 4) if which == 0 else (2, 5)
                g = (mine + got[j, single].astype(F32) + got[j, summed].astype(F32)).astype(BF16)
                out[j, which * half : (which + 1) * half, :] = g
                g = g.astype(F32)
                total[...] += jnp.sum((g * g).reshape(half // 8, 8, g.shape[-1]), axis=0)
        for unit in range(6):
            for matrix in (0, 1):
                copy(j, unit, matrix).wait_send()

    if deep:
        dgu_out = lambda j: pltpu.make_async_copy(dgu, dgu_o.at[:, rows(j, 2 * hidden)], dsem.at[0])
        flat_in = lambda j: pltpu.make_async_copy(gu_h.at[j], flat.at[:, j * 2 * hidden : (j + 1) * 2 * hidden], fsem.at[j])

    def chunk(j, _):
        s, slot = lax.rem(j, 2), lax.rem(j, 3)
        for c in w_in(j):
            c.wait()

        @pl.when(j + 1 < chunks)
        def _():
            for c in w_in(j + 1):
                c.start()

        if deep:

            @pl.when(j >= 1)
            def _():
                dgu_out(j - 1).wait()

        def part(t, _):
            @pl.when(j == 0)
            def _():
                a_in(t).wait()
                dy_in(t).wait()

            r = rows(t, big)
            gu = dot(av[r, :], gw[s])
            dact = dot(dyv[r, :], dw[s], 1, 1).astype(BF16).astype(F32)
            gate, up = gu[:, :hidden], gu[:, hidden:]
            sig = jax.nn.sigmoid(gate)
            silu = gate * sig
            act[r, :] = (silu * up).astype(BF16)
            dgu[r, hidden:] = (dact * silu).astype(BF16)
            dgu[r, :hidden] = (dact * up * (sig + silu * (1 - sig))).astype(BF16)
            return 0

        lax.fori_loop(0, parts, part, 0)
        if deep:
            dgu_out(j).start()

        @pl.when(j == 0)
        def _():
            for c in late:
                c.wait()

        tg[slot] = dot(atv[...], dgu[...]).astype(BF16)
        td[slot] = dot(dytv[...], act[...]).T.astype(BF16)

        @pl.when(j >= 1)
        def _():
            pass_on(j - 1)

        send_terms(j)

        @pl.when(j >= 2)
        def _():
            settle(j - 2)

        return 0

    if deep:
        for j in range(chunks):
            flat_in(j).start()
    lax.fori_loop(0, chunks, chunk, 0)
    last = chunks - 1
    if deep:
        for j in range(chunks):
            flat_in(j).wait()
        dgu_out(last).wait()
        tile = wide.shape[1]
        tiles = tokens // tile

        def ins(t):
            s = lax.rem(t, 2)
            return (
                pltpu.make_async_copy(dgu_o.at[rows(t, tile)], wide.at[s], psem.at[s, 0]),
                pltpu.make_async_copy(extra.at[rows(t, tile)], hst.at[s], psem.at[s, 1]),
            )

        def outs(t):
            s = lax.rem(t, 2)
            return (
                pltpu.make_async_copy(dyv.at[rows(t, tile)], dx_o.at[rows(t, tile)], osem.at[s, 0]),
                pltpu.make_async_copy(xtst.at[s], dxt_o.at[:, rows(t, tile)], osem.at[s, 1]),
            )

        for c in ins(0):
            c.start()

        def part(t, _):
            s = lax.rem(t, 2)
            for c in ins(t):
                c.wait()

            @pl.when(t + 1 < tiles)
            def _():
                for c in ins(t + 1):
                    c.start()

            @pl.when(t >= 2)
            def _():
                for c in outs(t):
                    c.wait()

            da = dot(wide[s], flat[...], 1, 1).astype(BF16).astype(F32)
            h = hst[s].astype(F32)
            scale = lax.rsqrt(jnp.mean(h * h, -1, keepdims=True) + 1e-6)
            along = jnp.sum(da * h, -1, keepdims=True) * (scale * scale * scale * (1.0 / dim))
            dh = (da * scale - h * along).astype(BF16)
            dx = (dyv[rows(t, tile), :].astype(F32) + dh.astype(F32)).astype(BF16)
            dyv[rows(t, tile), :] = dx
            xtst[s] = dx.T
            for c in outs(t):
                c.start()

            @pl.when(t == tiles // 4)
            def _():
                settle(last - 1)

            @pl.when(t == tiles // 2)
            def _():
                pass_on(last)

            return 0

        lax.fori_loop(0, tiles, part, 0)
        for t in (tiles - 2, tiles - 1):
            for c in outs(t):
                c.wait()
    else:
        settle(last - 1)
        pass_on(last)
    settle(last)

    total = sum(sqg[:, i * 128 : (i + 1) * 128] for i in range(sqg.shape[1] // 128))
    total += sum(sqd[:, i * 128 : (i + 1) * 128] for i in range(sqd.shape[1] // 128))
    if deep:
        sq[...] = total
    else:
        tot[me] = total + extra[...]
        peers = (left, right, across)

        def share_out(k):
            return remote(tot.at[me], tot.at[me], csem.at[0, k], csem.at[1, k], {"dp": peers[k]})

        for k in range(3):
            share_out(k).start()
    if not deep:
        for k in range(3):
            share_out(k).wait_send()
            share_out(k).wait_recv()
        sq[...] = tot[0] + tot[1] + tot[2] + tot[3]


def backward(n, deep, a, at_, dy, dyt, gu, d, extra):
    tokens, dim = a.shape
    chunks, hidden = d.shape[1:3]
    own, share = dim // n, hidden // n
    V = pltpu.VMEM
    S = jax.ShapeDtypeStruct
    tile = 256
    out_shape = [S((chunks, own, 2 * hidden), BF16), S((chunks, share, dim), BF16), S((8, 128), F32)]
    out_specs = [IN_VMEM] * 3
    scratch = [
        V((tokens, dim), BF16), V((dim, tokens), BF16), V((tokens, dim), BF16), V((dim, tokens), BF16),
        V((tokens, 2 * hidden), BF16), V((tokens, hidden), BF16), V((2, dim, 2 * hidden), BF16), V((2, hidden, dim), BF16),
        V((3, dim, 2 * hidden), BF16), V((3, hidden, dim), BF16),
        V((chunks, 6, own // 2, 2 * hidden), BF16), V((chunks, 6, share // 2, dim), BF16),
        V((8, 2 * hidden), F32), V((8, dim), F32),
        DMA((chunks, 12)), DMA((chunks, 12)), DMA((3, tokens // 1024)), DMA((2, 2)),
    ]
    if deep:
        out_shape += [S((tokens, chunks * 2 * hidden), BF16), S((tokens, dim), BF16), S((dim, tokens), BF16)]
        out_specs += [ANY] * 3
        scratch += [
            V((dim, chunks * 2 * hidden), BF16), V((2, tile, chunks * 2 * hidden), BF16), V((2, tile, dim), BF16),
            V((2, dim, tile), BF16), DMA((1,)), DMA((chunks,)), DMA((2, 2)), DMA((2, 2)),
        ]
    else:
        scratch += [V((n, 8, 128), F32), DMA((2, 3))]
    return pl.pallas_call(
        functools.partial(backward_kernel, n, deep),
        out_shape=out_shape,
        in_specs=[ANY] * 6 + [ANY if deep else IN_VMEM],
        out_specs=out_specs,
        scratch_shapes=scratch,
        compiler_params=pltpu.CompilerParams(collective_id=1 if deep else 2, has_side_effects=True, vmem_limit_bytes=63 * MIB),
        name="backward_deep" if deep else "backward_first",
    )(a, at_, dy, dyt, gu, d, extra)


def update_kernel(n, count, sq, g0, g1, d0, d1, wg, wu, wd, mg, mu, md, vg, vu, vd, *outs):
    factor = jnp.minimum(1.0, 0.5 * lax.rsqrt(jnp.sum(sq[...], keepdims=True) / count + 1e-30))
    first = pl.program_id(0) == 0
    gu = jnp.where(first, g0[...], g1[...]).astype(F32)
    chunks, hidden = gu.shape[0], gu.shape[2] // 2
    share = hidden // n

    def ordered(start):
        return jnp.concatenate([gu[j, :, start + o * share : start + (o + 1) * share] for o in range(n) for j in range(chunks)], -1)

    grads = (ordered(0), ordered(hidden), jnp.where(first, d0[...], d1[...]).astype(F32))
    for i, (g, w, m, v) in enumerate(zip(grads, (wg, wu, wd), (mg, mu, md), (vg, vu, vd), strict=True)):
        g = g * factor
        new_m = 0.9 * m[0] + 0.1 * g
        new_v = 0.95 * v[0] + 0.05 * g * g
        step = new_m * lax.rsqrt(new_v + 1e-8) + 0.1 * w[0].astype(F32)
        outs[i][0] = (w[0].astype(F32) - 0.02 * step).astype(BF16)
        outs[3 + i][0] = new_m
        outs[6 + i][0] = new_v


def update(n, sq, g0, g1, d0, d1, weights, m, v):
    layers, own, units = weights[0].shape
    down, dim = weights[2].shape[1:]
    chunks = g0.shape[0]
    cut = 4
    count = float(n * sum(w.size for w in weights))
    up = pl.BlockSpec((1, own // cut, units), lambda i, k: (i, k, 0))
    dn = pl.BlockSpec((1, down // cut, dim), lambda i, k: (i, k, 0))
    gs = lambda which: pl.BlockSpec((chunks, own // cut, g0.shape[2]), lambda i, k: (0, jnp.where(i == which, k, (cut - 1) * (1 - which)), 0))
    ds = lambda which: pl.BlockSpec((down // cut, dim), lambda i, k: (jnp.where(i == which, k, (cut - 1) * (1 - which)), 0))
    three = [up, up, dn]
    return pl.pallas_call(
        functools.partial(update_kernel, n, count),
        grid=(layers, cut),
        out_shape=[jax.ShapeDtypeStruct(w.shape, t) for t in (BF16, F32, F32) for w in weights],
        in_specs=[pl.BlockSpec((8, 128), lambda i, k: (0, 0)), gs(0), gs(1), ds(0), ds(1)] + three * 3,
        out_specs=three * 3,
        compiler_params=pltpu.CompilerParams(vmem_limit_bytes=60 * MIB),
        name="update",
    )(sq, g0, g1, d0.reshape(down, dim), d1.reshape(down, dim), *weights, *m, *v)


def solution(mesh):
    n = mesh.shape["dp"]

    def step(x, dy, *arrays):
        weights, m, v = (arrays[i : i + 3] for i in (0, 3, 6))
        gu, d, a0, a0t, dyt, h1, a1, a1t = forward(n, x[0], dy[0], *weights)
        g1, d1, sq1, _, dx, dxt = backward(n, True, a1, a1t, dy[0], dyt, gu, d, h1)
        g0, d0, sq = backward(n, False, a0, a0t, dx, dxt, gu, d, sq1)
        return tuple(update(n, sq, g0, g1, d0, d1, weights, m, v))

    states, cut = P(("rep", "dp"), None, None), P(None, "dp", None)
    return jax.shard_map(
        step,
        mesh=mesh,
        in_specs=(states, states) + (cut,) * 9,
        out_specs=(P("rep", "dp", None),) * 9,
        check_vma=False,
    )
```

time: 587 us -> 338 us (0.58); the launches traced: 580 us -> 337 us
  matrix products: 357 us -> 0 us
  Pallas kernels: 0 us -> 337 us
  waiting for transfers between devices: 134 us -> 0 us
  other arithmetic: 34.7 us -> 0 us
  local copies, waits for them, and re-layouts: 27.1 us -> 0 us
  between operations: 17.5 us -> 0.85 us
  blocking collectives: 9.14 us -> 0 us
    dot_general x15 -> x0, matrix products: 357 us -> none  [the longest x5 129 us: layer(): gate = jnp.dot(a, w['w_gate'], preferred_element_type=jnp.float32)]
    pallas_call x0 -> x4, Pallas kernels: none -> 337 us  [the longest x2 230 us: backward(): pl.pallas_call(functools.partial(backward_kernel, n, deep), out_shape=out...]
    all_gather x6 -> x0, waiting for transfers between devices: 67.9 us -> none  [fetched(): lax.all_gather(w[number], 'dp', axis=0, tiled=True)]
    reduce_scatter x6 -> x0, waiting for transfers between devices: 63.8 us -> none  [step(): lax.psum_scatter(by_w[name], 'dp', scatter_dimension=0, tiled=True)]
    unnamed x40 -> x0, local copies, waits for them, and re-layouts: 20.9 us -> none
    convert_element_type x2 -> x0, other arithmetic: 12.9 us -> none  [adamw(): return ((w - 0.02 * step).astype(jnp.bfloat16), m, v)]
    reduce_sum x4 -> x0, other arithmetic: 12.1 us -> none  [the longest x3 8.05 us: step(): squares = lax.psum(sum((jnp.sum(g * g) for g in gradients)), 'dp')]
    add_any x1 -> x0, other arithmetic: 9.67 us -> none  [normed(): wide = h.astype(jnp.float32)]
  transfers between devices with their start and end apart: 12 -> 0, of which waited for: 9 -> 0; matrix products, arithmetic and copies ran while one was open for 58% -> 0% of each run, Pallas kernels for 0% -> 0%
where the time goes in v1:
time: 338 us; the launch traced here: 337 us
  Pallas kernels  337 us (100%)
    pallas_call x2, Pallas kernels, backward(): pl.pallas_call(functools.partial(backward_kernel, n, deep), out_shape=out...  230 us
    pallas_call x1, Pallas kernels, forward(): pl.pallas_call(functools.partial(forward_kernel, n), out_shape=[S((layers...  88.8 us
    pallas_call x1, Pallas kernels, update(): pl.pallas_call(functools.partial(update_kernel, n, count), grid=(layers,...  17.3 us

profile of v1, /device:TPU:112, one launch (start us, length us, event | category | flops | bytes accessed | tf_op | source)
XLA Modules:
  0.0 337.4 jit_solution(8366343630904051089)
XLA Ops:
  0.6 88.8 %forward.1 = (bf16[2,7,768,512]{3,2,1,0:T(8,128)(2,1)}, bf16[2,7,256,768]{3,2,1,0:T(8,128)(2,1)}, bf16[4096,768]{1,0:T(8,128)(2,1)}, bf16[768,4096]{1,0:T(8,128)...) custom-call(bf16[4096,768]{1,0:T(8,128)(2,1)} %bitcast.6, ...), custom_call_target="tpu_custom_call" | custom-call | tf_op jit(solution)/shard_map/forward/pallas_call | solution.py:263
  89.5 122.9 %backward_deep.1 = (bf16[7,192,512]{2,1,0:T(8,128)(2,1)}, bf16[7,64,768]{2,1,0:T(8,128)(2,1)}, f32[8,128]{1,0:T(8,128)}, bf16[4096,3584]{1,0:T(8,128)(2,1)}, bf1...) custom-call(bf16[4096,768]{1,0:T(8,128)(2,1)} %get-tuple-element.27.refs_0_, ...), custom_call_target="tpu_custom_call" | custom-call | tf_op jit(solution)/shard_map/backward_deep/pallas_call | solution.py:556
  212.3 107.6 %backward_first.1 = (bf16[7,192,512]{2,1,0:T(8,128)(2,1)}, bf16[7,64,768]{2,1,0:T(8,128)(2,1)}, f32[8,128]{1,0:T(8,128)}) custom-call(bf16[4096,768]{1,0:T(8,128)(2,1)} %get-tuple-element.25.refs_0_, bf16[768,4096]{1,0:T(8,128)(2,1)} %get-tuple-element.26.refs_1_, bf16[4096,768]{1,0:T(8,128)(2,1)} %get-tuple-element.33.refs_2_, ...), custom_call_target="tpu_custom_call" | custom-call | tf_op jit(solution)/shard_map/backward_first/pallas_call | solution.py:556
  319.9 17.3 %update.1 = (bf16[2,192,1792]{2,1,0:T(8,128)(2,1)}, bf16[2,192,1792]{2,1,0:T(8,128)(2,1)}, bf16[2,448,768]{2,1,0:T(8,128)(2,1)}, f32[2,192,1792]{2,1,0:T(8,128)}...) custom-call(f32[8,128]{1,0:T(8,128)} %get-tuple-element.36.sq, ...), custom_call_target="tpu_custom_call" | custom-call | tf_op jit(solution)/shard_map/update/pallas_call | solution.py:599

commit v2 on v1

--- a/solution.py
+++ b/solution.py
@@ -39,11 +39,13 @@
     return me, lax.rem(me + n - 1, n), lax.rem(me + 1, n), lax.rem(me + 2, n)
 
 
+def greet(where):
+    for device in where:
+        pl.semaphore_signal(pltpu.get_barrier_semaphore(), inc=1, device_id=device, device_id_type=MESH)
+
+
 def meet(where):
-    barrier = pltpu.get_barrier_semaphore()
-    for device in where:
-        pl.semaphore_signal(barrier, inc=1, device_id=device, device_id_type=MESH)
-    pl.semaphore_wait(barrier, len(where))
+    pl.semaphore_wait(pltpu.get_barrier_semaphore(), len(where))
 
 
 def remote(source, target, send, receive, device):
@@ -56,13 +58,13 @@
 
 
 def forward_kernel(
-    n, x_h, dy_h, wg, wu, wd, gu_o, d_o, a_o, at_o, dyt_o, h_o, a1_o, a1t_o,
-    xv, av, dyv, acts, gw, dw, packed, tst, tst2, hst, ast, ssem, rsem, xsem, dysem, osem, wsem,
+    n, x_h, dy_h, wg, wu, wd, gu_o, d_o, kept_o, at_o, dyt_o, h_o, a1_o, a1t_o,
+    xv, av, dyv, acts, gw, dw, gst, tst, tst2, hst, ast, ssem, rsem, xsem, dysem, osem, wsem, ksem,
 ):
     layers, chunks = gw.shape[0], gw.shape[1]
     tokens, dim = xv.shape
     own, hidden = wg.shape[1], dw.shape[2]
-    share, third = wd.shape[1] // chunks, own // 4
+    share, piece = wd.shape[1] // chunks, own // 4
     steps = layers * chunks
     tile = dyv.shape[1]
     tiles = tokens // tile
@@ -71,6 +73,9 @@
     core, side = lax.rem(rep, 2), lax.rem(rep // 2, 2)
     mate, twin = rep + 1 - 2 * core, rep + 2 - 4 * side
 
+    friends = [{"dp": left}, {"dp": right}, {"rep": mate}, {"rep": twin}]
+    greet(friends)
+
     def x_in(t):
         return pltpu.make_async_copy(x_h.at[rows(t, tile)], xv.at[rows(t, tile)], xsem.at[t])
 
@@ -85,24 +90,25 @@
     dy_in(0).start()
     dy_in(1).start()
 
-    for layer in range(layers):
+    def pack(layer):
         gate, up = wg[layer], wu[layer]
         for j in range(chunks):
             pieces = [w[:, o * share * chunks + j * share : o * share * chunks + (j + 1) * share] for w in (gate, up) for o in range(n)]
-            packed[layer * chunks + j] = jnp.concatenate(pieces, -1)
+            start = (layer * chunks + j) * own
+            acts[start : start + own, : 2 * hidden] = jnp.concatenate(pieces, -1)
 
     def place(s, _):
         layer, j = s // chunks, lax.rem(s, chunks)
-        gw[layer, j, at(me * own, own), :] = packed[s]
+        gw[layer, j, at(me * own, own), :] = acts[rows(s, own), : 2 * hidden]
         dw[layer, j, at(me * share, share), :] = wd[layer, rows(j, share), :]
         return 0
 
-    lax.fori_loop(0, steps, place, 0)
-
-    meet([{"dp": left}, {"dp": right}, {"rep": mate}, {"rep": twin}])
+    pack(0)
+    lax.fori_loop(0, chunks, place, 0)
+    meet(friends)
 
     def up_part(s, owner, which):
-        return gw.at[s // chunks, lax.rem(s, chunks), at(owner * own + which * 2 * third + core * third, third), :]
+        return gw.at[s // chunks, lax.rem(s, chunks), at(owner * own + which * 2 * piece + core * piece, piece), :]
 
     def down_part(s, owner):
         return dw.at[s // chunks, lax.rem(s, chunks), at(owner * share + core * (share // 2), share // 2), :]
@@ -134,24 +140,34 @@
         )
 
     def stage(s, wait, begin):
-        @pl.when((s >= 0) & (s < steps))
+        @pl.when(s < steps)
         def _():
             for kind in wait:
                 copy(s, kind).wait_recv()
             for kind in begin:
                 copy(s, kind).start()
 
-    def tick(k):
-        stage(k + 1, (), (0, 1, 2, 3))
-        stage(k - 1, (0, 1, 2, 3), (4, 5, 6, 7, 9, 10, 11, 12))
-        stage(k - 2, (4, 5), (8, 13, 14))
-        stage(k - 3, (6, 7, 8), (15, 16, 17))
-        stage(k - 4, range(9, KINDS), ())
-
-        @pl.when((k >= 4) & (k - 4 < steps))
+    first = ((), (0, 1, 2, 3))
+    second = ((0, 1, 2, 3), (4, 5, 6, 7, 9, 10, 11, 12))
+    third = ((4, 5), (8, 13, 14))
+    fourth = ((6, 7, 8), (15, 16, 17))
+
+    def arrived(s):
+        stage(s, range(9, KINDS), ())
+
+        @pl.when(s < steps)
         def _():
-            for c in weights_out(k - 4):
+            for c in weights_out(s):
                 c.start()
+
+    def half_way(j):
+        stage(j + 1, *fourth)
+        stage(j + 4, *second)
+        stage(j + 6, *first)
+
+    def at_end(j):
+        stage(j + 3, *third)
+        arrived(j + 1)
 
     def at_out(t, slot):
         return pltpu.make_async_copy(tst.at[slot], at_o.at[:, rows(t, tile)], osem.at[slot, 0])
@@ -163,8 +179,7 @@
         x_in(t).wait()
         dy_in(t).wait()
 
-        @pl.when(t >= 2)
-        def _():
+        if t >= 2:
             at_out(t, slot).wait()
             dyt_out(t, slot).wait()
 
@@ -175,39 +190,53 @@
         at_out(t, slot).start()
         dyt_out(t, slot).start()
 
-        @pl.when(t + 2 < tiles)
-        def _():
+        if t + 2 < tiles:
             dy_in(t + 2).start()
 
-    stage(0, (), (0, 1, 2, 3))
-
-    def open_(k, _):
-        tick(k)
-        prepare(2 * k, 0)
-        prepare(2 * k + 1, 1)
-        return 0
-
-    lax.fori_loop(0, 4, open_, 0)
-    tick(4)
-    a_out = pltpu.make_async_copy(av, a_o, osem.at[0, 2])
-    a_out.start()
+    stage(0, *first)
+    stage(1, *first)
+    pack(1)
+    lax.fori_loop(chunks, steps, place, 0)
+    prepare(0, 0)
+    prepare(1, 1)
+    order = ((0, second), (2, first), 2, (1, second), (3, first), 3, (0, third), 4, (2, second), (4, first), 5, (1, third), 6, (0, fourth), 7)
+    for item in order + ((3, second), (5, first), (2, third)):
+        if isinstance(item, int):
+            prepare(item, item % 2)
+        else:
+            stage(item[0], *item[1])
+    arrived(0)
     big = 2 * tile
+    parts = tokens // big
+
+    def keep(j, t):
+        return pltpu.make_async_copy(gst.at[lax.rem(t, 2)], kept_o.at[j, rows(t, big)], ksem.at[lax.rem(t, 2)])
 
     def chunk(j, _):
         def part(t, _):
+            @pl.when((j > 0) | (t >= 2))
+            def _():
+                keep(j, t).wait()
+
+            slot = lax.rem(t, 2)
             gu = dot(av[rows(t, big), :], gw[0, j])
+            gst[slot] = gu
+            keep(j, t).start()
             gate, up = gu[:, :hidden], gu[:, hidden:]
             acts[rows(t, big), rows(j, hidden)] = (gate * jax.nn.sigmoid(gate) * up).astype(BF16)
             return 0
 
-        lax.fori_loop(0, tokens // big, part, 0)
-        tick(j + 5)
+        lax.fori_loop(0, parts // 2, part, 0)
+        half_way(j)
+        lax.fori_loop(parts // 2, parts, part, 0)
+        at_end(j)
         return 0
 
     lax.fori_loop(0, chunks, chunk, 0)
     for slot in range(2):
         at_out(0, slot).wait()
         dyt_out(0, slot).wait()
+        keep(chunks - 1, slot).wait()
 
     def outs(t):
         slot = lax.rem(t, 2)
@@ -219,6 +248,8 @@
 
     def close(t, _):
         slot = lax.rem(t, 2)
+
+        half_way(chunks + t)
 
         @pl.when(t >= 2)
         def _():
@@ -233,14 +264,13 @@
         tst[slot] = a.T
         for c in outs(t):
             c.start()
-        tick(chunks + 5 + t)
+        at_end(chunks + t)
         return 0
 
     lax.fori_loop(0, tiles, close, 0)
     for t in (tiles - 2, tiles - 1):
         for c in outs(t):
             c.wait()
-    a_out.wait()
 
     def finish(s, _):
         for kind in range(KINDS):
@@ -264,7 +294,7 @@
         functools.partial(forward_kernel, n),
         out_shape=[
             S((layers, chunks, dim, 2 * hidden), BF16), S((layers, chunks, hidden, dim), BF16),
-            S((tokens, dim), BF16), S((dim, tokens), BF16), S((dim, tokens), BF16),
+            S((chunks, tokens, 2 * hidden), F32), S((dim, tokens), BF16), S((dim, tokens), BF16),
             S((tokens, dim), BF16), S((tokens, dim), BF16), S((dim, tokens), BF16),
         ],
         in_specs=[ANY, ANY, IN_VMEM, IN_VMEM, IN_VMEM],
@@ -272,9 +302,9 @@
         scratch_shapes=[
             V((tokens, dim), BF16), V((tokens, dim), BF16), V((2, tile, dim), BF16), V((tokens, units), BF16),
             V((layers, chunks, dim, 2 * hidden), BF16), V((layers, chunks, hidden, dim), BF16),
-            V((layers * chunks, own, 2 * hidden), BF16), V((2, dim, tile), BF16), V((2, dim, tile), BF16), V((2, tile, dim), BF16), V((2, tile, dim), BF16),
+            V((2, 2 * tile, 2 * hidden), F32), V((2, dim, tile), BF16), V((2, dim, tile), BF16), V((2, tile, dim), BF16), V((2, tile, dim), BF16),
             DMA((layers * chunks, KINDS)), DMA((layers * chunks, KINDS)),
-            DMA((tokens // tile,)), DMA((2,)), DMA((2, 6)), DMA((layers * chunks, 2)),
+            DMA((tokens // tile,)), DMA((2,)), DMA((2, 6)), DMA((layers * chunks, 2)), DMA((2,)),
         ],
         compiler_params=pltpu.CompilerParams(collective_id=0, has_side_effects=True, vmem_limit_bytes=63 * MIB),
         name="forward",
@@ -284,17 +314,19 @@
 def backward_kernel(n, deep, *refs):
     it = iter(refs)
     take = lambda count: [next(it) for _ in range(count)]
-    a_h, at_h, dy_h, dyt_h, gu_all, d_all, extra = take(7)
-    gu_h, d_h = gu_all.at[1 if deep else 0], d_all.at[1 if deep else 0]
+    a_h, at_h, dy_h, dyt_h, d_all, extra = take(6)
+    d_h = d_all.at[1 if deep else 0]
+    if deep:
+        gu_h = next(it).at[1]
     og, od, sq = take(3)
     if deep:
         dgu_o, dx_o, dxt_o = take(3)
-    av, atv, dyv, dytv, dgu, act, gw, dw, tg, td, rg, rd, sqg, sqd, ssem, rsem, isem, wsem = take(18)
+    av, atv, dyv, dytv, dgu, act, dw, tg, td, rg, rd, sqg, sqd, ssem, rsem, isem, wsem = take(17)
     if deep:
-        flat, wide, hst, xtst, dsem, fsem, psem, osem = take(8)
+        gw, flat, wide, hst, xtst, dsem, fsem, psem, osem = take(9)
     else:
         tot, csem = take(2)
-    tokens, dim = av.shape
+    tokens, dim = dyv.shape
     chunks, hidden = d_all.shape[1:3]
     own, share = dim // n, hidden // n
     g2, d2 = own // 2, share // 2
@@ -305,72 +337,85 @@
     def a_in(t):
         return pltpu.make_async_copy(a_h.at[rows(t, big)], av.at[rows(t, big)], isem.at[0, t])
 
+    def kept_in(j, t):
+        return pltpu.make_async_copy(a_h.at[j, rows(t, big)], av.at[t], isem.at[0, t])
+
     def dy_in(t):
         return pltpu.make_async_copy(dy_h.at[rows(t, big)], dyv.at[rows(t, big)], isem.at[1, t])
 
-    late = (pltpu.make_async_copy(at_h, atv, isem.at[2, 0]), pltpu.make_async_copy(dyt_h, dytv, isem.at[2, 1]))
+    late = (pltpu.make_async_copy(dyt_h, dytv, isem.at[2, 0]), pltpu.make_async_copy(at_h, atv, isem.at[2, 1]))
 
     def w_in(j):
         s = lax.rem(j, 2)
-        return (pltpu.make_async_copy(gu_h.at[j], gw.at[s], wsem.at[s, 0]), pltpu.make_async_copy(d_h.at[j], dw.at[s], wsem.at[s, 1]))
-
+        copies = [pltpu.make_async_copy(d_h.at[j], dw.at[s], wsem.at[s, 1])]
+        if deep:
+            copies.append(pltpu.make_async_copy(gu_h.at[j], gw.at[s], wsem.at[s, 0]))
+        return copies
+
+    friends = [{"dp": left}, {"dp": right}] + ([] if deep else [{"dp": across}])
+    greet(friends)
     for c in w_in(0):
         c.start()
-    for t in range(parts):
-        a_in(t).start()
+    if not deep:
+        for t in range(parts):
+            kept_in(0, t).start()
+    for t in range(2):
         dy_in(t).start()
-    for c in late:
-        c.start()
+        if deep:
+            a_in(t).start()
     sqg[...] = jnp.zeros_like(sqg)
     sqd[...] = jnp.zeros_like(sqd)
-    meet([{"dp": left}, {"dp": right}] + ([] if deep else [{"dp": across}]))
+    meet(friends)
+
+    def spot(j, matrix, owner, which):
+        if matrix < 2:
+            return tg, (lax.rem(j, 3), matrix, at(owner * own + which * g2, g2))
+        return td, (lax.rem(j, 3), at(owner * share + which * d2, d2))
+
+    def landing(j, unit, matrix):
+        return (rg, (j, unit, matrix)) if matrix < 2 else (rd, (j, unit))
 
     def copy(j, unit, matrix):
-        slot = lax.rem(j, 3)
-        term, half, block = (tg, g2, own) if matrix == 0 else (td, d2, share)
-        device = {"dp": right if unit % 2 == 0 else left}
-        if unit < 2:
-            source = term.at[slot, at(across * block + unit * half, half), :]
-        elif unit < 4:
-            owner, which = (right, 1) if unit == 2 else (left, 0)
-            source = term.at[slot, at(owner * block + which * half, half), :]
-        else:
-            owner, which = (right, 0) if unit == 4 else (left, 1)
-            source = term.at[slot, at(owner * block + which * half, half), :]
-        target = (rg if matrix == 0 else rd).at[j, unit]
-        return remote(source, target, ssem.at[j, 2 * unit + matrix], rsem.at[j, 2 * unit + matrix], device)
-
-    def send_terms(j):
+        owner, which = ((across, 0), (across, 1), (right, 1), (left, 0), (right, 0), (left, 1))[unit]
+        source, place = spot(j, matrix, owner, which)
+        target, index = landing(j, unit, matrix)
+        sem = 3 * unit + matrix
+        return remote(source.at[place], target.at[index], ssem.at[j, sem], rsem.at[j, sem], {"dp": right if unit % 2 == 0 else left})
+
+    def send_terms(j, matrix):
         for unit in (0, 1, 2, 3):
-            for matrix in (0, 1):
-                copy(j, unit, matrix).start()
-
-    def pass_on(j):
-        slot = lax.rem(j, 3)
-        for unit in (0, 1):
-            owner = right if unit == 0 else left
-            for matrix, (term, half, block, got) in enumerate(((tg, g2, own, rg), (td, d2, share, rd))):
-                copy(j, unit, matrix).wait_recv()
-                place = at(owner * block + unit * half, half)
-                term[slot, place, :] = (term[slot, place, :].astype(F32) + got[j, unit].astype(F32)).astype(BF16)
-                copy(j, unit + 4, matrix).start()
-
-    def settle(j):
-        slot = lax.rem(j, 3)
+            copy(j, unit, matrix).start()
+
+    def pass_on(j, matrix):
+        for unit, owner, which in ((0, right, 0), (1, left, 1)):
+            copy(j, unit, matrix).wait_recv()
+            term, place = spot(j, matrix, owner, which)
+            got, index = landing(j, unit, matrix)
+            term[place] = (term[place].astype(F32) + got[index].astype(F32)).astype(BF16)
+            copy(j, unit + 4, matrix).start()
+
+    def settle(j, matrix):
         for unit in (2, 3, 4, 5):
-            for matrix in (0, 1):
-                copy(j, unit, matrix).wait_recv()
-        for matrix, (term, half, block, got, out, total) in enumerate(((tg, g2, own, rg, og, sqg), (td, d2, share, rd, od, sqd))):
-            for which in (0, 1):
-                mine = term[slot, at(me * block + which * half, half), :].astype(F32)
-                single, summed = (3, 4) if which == 0 else (2, 5)
-                g = (mine + got[j, single].astype(F32) + got[j, summed].astype(F32)).astype(BF16)
-                out[j, which * half : (which + 1) * half, :] = g
-                g = g.astype(F32)
-                total[...] += jnp.sum((g * g).reshape(half // 8, 8, g.shape[-1]), axis=0)
+            copy(j, unit, matrix).wait_recv()
+        for which, single, summed in ((0, 3, 4), (1, 2, 5)):
+            term, place = spot(j, matrix, me, which)
+            got, one = landing(j, single, matrix)
+            _, other = landing(j, summed, matrix)
+            g = (term[place].astype(F32) + got[one].astype(F32) + got[other].astype(F32)).astype(BF16)
+            if matrix < 2:
+                og[j, which * g2 : (which + 1) * g2, matrix * hidden : (matrix + 1) * hidden] = g
+            else:
+                od[j, which * d2 : (which + 1) * d2, :] = g
+            g = g.astype(F32)
+            total = sqg if matrix < 2 else sqd
+            total[...] += jnp.sum((g * g).reshape(g.shape[0] // 8, 8, g.shape[1]), axis=0)
         for unit in range(6):
-            for matrix in (0, 1):
-                copy(j, unit, matrix).wait_send()
+            copy(j, unit, matrix).wait_send()
+
+    def when(condition, what, *args):
+        @pl.when(condition)
+        def _():
+            what(*args)
 
     if deep:
         dgu_out = lambda j: pltpu.make_async_copy(dgu, dgu_o.at[:, rows(j, 2 * hidden)], dsem.at[0])
@@ -395,11 +440,25 @@
         def part(t, _):
             @pl.when(j == 0)
             def _():
-                a_in(t).wait()
                 dy_in(t).wait()
+                if deep:
+                    a_in(t).wait()
+
+                @pl.when(t + 2 < parts)
+                def _():
+                    dy_in(t + 2).start()
+                    if deep:
+                        a_in(t + 2).start()
+
+                for i in range(2):
+                    when(t == parts - 2 + i, late[i].start)
 
             r = rows(t, big)
-            gu = dot(av[r, :], gw[s])
+            if deep:
+                gu = dot(av[r, :], gw[s])
+            else:
+                kept_in(j, t).wait()
+                gu = av[t]
             dact = dot(dyv[r, :], dw[s], 1, 1).astype(BF16).astype(F32)
             gate, up = gu[:, :hidden], gu[:, hidden:]
             sig = jax.nn.sigmoid(gate)
@@ -407,35 +466,37 @@
             act[r, :] = (silu * up).astype(BF16)
             dgu[r, hidden:] = (dact * silu).astype(BF16)
             dgu[r, :hidden] = (dact * up * (sig + silu * (1 - sig))).astype(BF16)
+            if not deep:
+                when(j + 1 < chunks, lambda: kept_in(j + 1, t).start())
             return 0
 
         lax.fori_loop(0, parts, part, 0)
         if deep:
             dgu_out(j).start()
 
-        @pl.when(j == 0)
-        def _():
-            for c in late:
-                c.wait()
-
-        tg[slot] = dot(atv[...], dgu[...]).astype(BF16)
+            @pl.when(j == chunks - 2)
+            def _():
+                for i in range(chunks):
+                    flat_in(i).start()
+
+        when(j == 0, late[0].wait)
         td[slot] = dot(dytv[...], act[...]).T.astype(BF16)
-
-        @pl.when(j >= 1)
-        def _():
-            pass_on(j - 1)
-
-        send_terms(j)
-
-        @pl.when(j >= 2)
-        def _():
-            settle(j - 2)
-
+        when(j == 0, late[1].wait)
+        if deep:
+            both = dot(atv[...], dgu[...]).astype(BF16)
+            tg[slot, 0] = both[:, :hidden]
+            tg[slot, 1] = both[:, hidden:]
+        else:
+            tg[slot, 0] = dot(atv[...], dgu[:, :hidden]).astype(BF16)
+            tg[slot, 1] = dot(atv[...], dgu[:, hidden:]).astype(BF16)
+        for matrix in (2, 0, 1):
+            when(j >= 1, pass_on, j - 1, matrix)
+        for matrix in (2, 0, 1):
+            send_terms(j, matrix)
+        for matrix in (2, 0, 1):
+            when(j >= 2, settle, j - 2, matrix)
         return 0
 
-    if deep:
-        for j in range(chunks):
-            flat_in(j).start()
     lax.fori_loop(0, chunks, chunk, 0)
     last = chunks - 1
     if deep:
@@ -490,11 +551,13 @@
 
             @pl.when(t == tiles // 4)
             def _():
-                settle(last - 1)
+                for matrix in (2, 0, 1):
+                    settle(last - 1, matrix)
 
             @pl.when(t == tiles // 2)
             def _():
-                pass_on(last)
+                for matrix in (2, 0, 1):
+                    pass_on(last, matrix)
 
             return 0
 
@@ -503,9 +566,13 @@
             for c in outs(t):
                 c.wait()
     else:
-        settle(last - 1)
-        pass_on(last)
-    settle(last)
+        pass_on(last, 2)
+        pass_on(last, 0)
+        for matrix in (2, 0, 1):
+            settle(last - 1, matrix)
+        pass_on(last, 1)
+    for matrix in (2, 0, 1):
+        settle(last, matrix)
 
     total = sum(sqg[:, i * 128 : (i + 1) * 128] for i in range(sqg.shape[1] // 128))
     total += sum(sqd[:, i * 128 : (i + 1) * 128] for i in range(sqd.shape[1] // 128))
@@ -527,28 +594,29 @@
         sq[...] = tot[0] + tot[1] + tot[2] + tot[3]
 
 
-def backward(n, deep, a, at_, dy, dyt, gu, d, extra):
-    tokens, dim = a.shape
+def backward(n, deep, a, at_, dy, dyt, d, extra, *gu):
+    tokens, dim = dy.shape
     chunks, hidden = d.shape[1:3]
     own, share = dim // n, hidden // n
     V = pltpu.VMEM
     S = jax.ShapeDtypeStruct
-    tile = 256
+    tile, big = 256, 1024
     out_shape = [S((chunks, own, 2 * hidden), BF16), S((chunks, share, dim), BF16), S((8, 128), F32)]
     out_specs = [IN_VMEM] * 3
     scratch = [
-        V((tokens, dim), BF16), V((dim, tokens), BF16), V((tokens, dim), BF16), V((dim, tokens), BF16),
-        V((tokens, 2 * hidden), BF16), V((tokens, hidden), BF16), V((2, dim, 2 * hidden), BF16), V((2, hidden, dim), BF16),
-        V((3, dim, 2 * hidden), BF16), V((3, hidden, dim), BF16),
-        V((chunks, 6, own // 2, 2 * hidden), BF16), V((chunks, 6, share // 2, dim), BF16),
-        V((8, 2 * hidden), F32), V((8, dim), F32),
-        DMA((chunks, 12)), DMA((chunks, 12)), DMA((3, tokens // 1024)), DMA((2, 2)),
+        V((tokens, dim), BF16) if deep else V((tokens // big, big, 2 * hidden), F32),
+        V((dim, tokens), BF16), V((tokens, dim), BF16), V((dim, tokens), BF16),
+        V((tokens, 2 * hidden), BF16), V((tokens, hidden), BF16), V((2, hidden, dim), BF16),
+        V((3, 2, dim, hidden), BF16), V((3, hidden, dim), BF16),
+        V((chunks, 6, 2, own // 2, hidden), BF16), V((chunks, 6, share // 2, dim), BF16),
+        V((8, hidden), F32), V((8, dim), F32),
+        DMA((chunks, 18)), DMA((chunks, 18)), DMA((3, tokens // big)), DMA((2, 2)),
     ]
     if deep:
         out_shape += [S((tokens, chunks * 2 * hidden), BF16), S((tokens, dim), BF16), S((dim, tokens), BF16)]
         out_specs += [ANY] * 3
         scratch += [
-            V((dim, chunks * 2 * hidden), BF16), V((2, tile, chunks * 2 * hidden), BF16), V((2, tile, dim), BF16),
+            V((2, dim, 2 * hidden), BF16), V((dim, chunks * 2 * hidden), BF16), V((2, tile, chunks * 2 * hidden), BF16), V((2, tile, dim), BF16),
             V((2, dim, tile), BF16), DMA((1,)), DMA((chunks,)), DMA((2, 2)), DMA((2, 2)),
         ]
     else:
@@ -556,12 +624,12 @@
     return pl.pallas_call(
         functools.partial(backward_kernel, n, deep),
         out_shape=out_shape,
-        in_specs=[ANY] * 6 + [ANY if deep else IN_VMEM],
+        in_specs=[ANY] * 5 + ([ANY, ANY] if deep else [IN_VMEM]),
         out_specs=out_specs,
         scratch_shapes=scratch,
         compiler_params=pltpu.CompilerParams(collective_id=1 if deep else 2, has_side_effects=True, vmem_limit_bytes=63 * MIB),
         name="backward_deep" if deep else "backward_first",
-    )(a, at_, dy, dyt, gu, d, extra)
+    )(a, at_, dy, dyt, d, extra, *gu)
 
 
 def update_kernel(n, count, sq, g0, g1, d0, d1, wg, wu, wd, mg, mu, md, vg, vu, vd, *outs):
@@ -612,9 +680,9 @@
 
     def step(x, dy, *arrays):
         weights, m, v = (arrays[i : i + 3] for i in (0, 3, 6))
-        gu, d, a0, a0t, dyt, h1, a1, a1t = forward(n, x[0], dy[0], *weights)
-        g1, d1, sq1, _, dx, dxt = backward(n, True, a1, a1t, dy[0], dyt, gu, d, h1)
-        g0, d0, sq = backward(n, False, a0, a0t, dx, dxt, gu, d, sq1)
+        gu, d, kept, a0t, dyt, h1, a1, a1t = forward(n, x[0], dy[0], *weights)
+        g1, d1, sq1, _, dx, dxt = backward(n, True, a1, a1t, dy[0], dyt, d, h1, gu)
+        g0, d0, sq = backward(n, False, kept, a0t, dx, dxt, d, sq1)
         return tuple(update(n, sq, g0, g1, d0, d1, weights, m, v))
 
     states, cut = P(("rep", "dp"), None, None), P(None, "dp", None)

time: 338 us -> 320 us (0.947)
  Pallas kernels: 337 us -> 319 us
    pallas_call x2, Pallas kernels: 230 us -> 219 us  [backward(): pl.pallas_call(functools.partial(backward_kernel, n, deep), out_shape=out...]
    pallas_call x1, Pallas kernels: 88.8 us -> 82.9 us  [forward(): pl.pallas_call(functools.partial(forward_kernel, n), out_shape=[S((layers...]
where the time goes in v2:
time: 320 us; the launch traced here: 319 us
  Pallas kernels  319 us (100%)
    pallas_call x2, Pallas kernels, backward(): pl.pallas_call(functools.partial(backward_kernel, n, deep), out_shape=out...  219 us
    pallas_call x1, Pallas kernels, forward(): pl.pallas_call(functools.partial(forward_kernel, n), out_shape=[S((layers...  82.9 us
    pallas_call x1, Pallas kernels, update(): pl.pallas_call(functools.partial(update_kernel, n, count), grid=(layers,...  17.3 us

profile of v2, /device:TPU:112, one launch (start us, length us, event | category | flops | bytes accessed | tf_op | source)
XLA Modules:
  0.0 319.5 jit_solution(13559552213057348243)
XLA Ops:
  0.6 82.9 %forward.1 = (bf16[2,7,768,512]{3,2,1,0:T(8,128)(2,1)}, bf16[2,7,256,768]{3,2,1,0:T(8,128)(2,1)}, f32[7,4096,512]{2,1,0:T(8,128)}, bf16[768,4096]{1,0:T(8,128)(2...) custom-call(bf16[4096,768]{1,0:T(8,128)(2,1)} %bitcast.6, ...), custom_call_target="tpu_custom_call" | custom-call | tf_op jit(solution)/shard_map/forward/pallas_call | solution.py:293
  83.5 123.2 %backward_deep.1 = (bf16[7,192,512]{2,1,0:T(8,128)(2,1)}, bf16[7,64,768]{2,1,0:T(8,128)(2,1)}, f32[8,128]{1,0:T(8,128)}, bf16[4096,3584]{1,0:T(8,128)(2,1)}, bf1...) custom-call(bf16[4096,768]{1,0:T(8,128)(2,1)} %get-tuple-element.27.refs_0_, ...), custom_call_target="tpu_custom_call" | custom-call | tf_op jit(solution)/shard_map/backward_deep/pallas_call | solution.py:624
  206.7 95.3 %backward_first.1 = (bf16[7,192,512]{2,1,0:T(8,128)(2,1)}, bf16[7,64,768]{2,1,0:T(8,128)(2,1)}, f32[8,128]{1,0:T(8,128)}) custom-call(f32[7,4096,512]{2,1,0:T(8,128)} %get-tuple-element.25.refs_0_, bf16[768,4096]{1,0:T(8,128)(2,1)} %get-tuple-element.26.refs_1_, bf16[4096,768]{1,0:T(8,128)(2,1)} %get-tuple-element.33.refs_2_, ...), custom_call_target="tpu_custom_call" | custom-call | tf_op jit(solution)/shard_map/backward_first/pallas_call | solution.py:624
  302.0 17.3 %update.1 = (bf16[2,192,1792]{2,1,0:T(8,128)(2,1)}, bf16[2,192,1792]{2,1,0:T(8,128)(2,1)}, bf16[2,448,768]{2,1,0:T(8,128)(2,1)}, f32[2,192,1792]{2,1,0:T(8,128)}...) custom-call(f32[8,128]{1,0:T(8,128)} %get-tuple-element.36.sq, ...), custom_call_target="tpu_custom_call" | custom-call | tf_op jit(solution)/shard_map/update/pallas_call | solution.py:667

commit v3 on v2

--- a/solution.py
+++ b/solution.py
@@ -210,18 +210,23 @@
     parts = tokens // big
 
     def keep(j, t):
-        return pltpu.make_async_copy(gst.at[lax.rem(t, 2)], kept_o.at[j, rows(t, big)], ksem.at[lax.rem(t, 2)])
+        slot = lax.rem(t, 2)
+        return [
+            pltpu.make_async_copy(gst.at[slot, rows(i, tile)], kept_o.at[j, rows(2 * t + i, tile)], ksem.at[slot, i]) for i in range(2)
+        ]
 
     def chunk(j, _):
         def part(t, _):
             @pl.when((j > 0) | (t >= 2))
             def _():
-                keep(j, t).wait()
+                for c in keep(j, t):
+                    c.wait()
 
             slot = lax.rem(t, 2)
             gu = dot(av[rows(t, big), :], gw[0, j])
             gst[slot] = gu
-            keep(j, t).start()
+            for c in keep(j, t):
+                c.start()
             gate, up = gu[:, :hidden], gu[:, hidden:]
             acts[rows(t, big), rows(j, hidden)] = (gate * jax.nn.sigmoid(gate) * up).astype(BF16)
             return 0
@@ -236,7 +241,8 @@
     for slot in range(2):
         at_out(0, slot).wait()
         dyt_out(0, slot).wait()
-        keep(chunks - 1, slot).wait()
+        for c in keep(chunks - 1, slot):
+            c.wait()
 
     def outs(t):
         slot = lax.rem(t, 2)
@@ -304,7 +310,7 @@
             V((layers, chunks, dim, 2 * hidden), BF16), V((layers, chunks, hidden, dim), BF16),
             V((2, 2 * tile, 2 * hidden), F32), V((2, dim, tile), BF16), V((2, dim, tile), BF16), V((2, tile, dim), BF16), V((2, tile, dim), BF16),
             DMA((layers * chunks, KINDS)), DMA((layers * chunks, KINDS)),
-            DMA((tokens // tile,)), DMA((2,)), DMA((2, 6)), DMA((layers * chunks, 2)), DMA((2,)),
+            DMA((tokens // tile,)), DMA((2,)), DMA((2, 6)), DMA((layers * chunks, 2)), DMA((2, 2)),
         ],
         compiler_params=pltpu.CompilerParams(collective_id=0, has_side_effects=True, vmem_limit_bytes=63 * MIB),
         name="forward",
@@ -343,7 +349,13 @@
     def dy_in(t):
         return pltpu.make_async_copy(dy_h.at[rows(t, big)], dyv.at[rows(t, big)], isem.at[1, t])
 
-    late = (pltpu.make_async_copy(dyt_h, dytv, isem.at[2, 0]), pltpu.make_async_copy(at_h, atv, isem.at[2, 1]))
+    def late(which):
+        source, target = ((dyt_h, dytv), (at_h, atv))[which]
+        return [
+            pltpu.make_async_copy(source.at[i * own : (i + 1) * own], target.at[i * own : (i + 1) * own], isem.at[2 + which, i])
+            for i in range(n)
+        ]
+
 
     def w_in(j):
         s = lax.rem(j, 2)
@@ -359,7 +371,7 @@
     if not deep:
         for t in range(parts):
             kept_in(0, t).start()
-    for t in range(2):
+    for t in range(parts):
         dy_in(t).start()
         if deep:
             a_in(t).start()
@@ -444,14 +456,15 @@
                 if deep:
                     a_in(t).wait()
 
-                @pl.when(t + 2 < parts)
+                @pl.when(t < 2)
                 def _():
-                    dy_in(t + 2).start()
-                    if deep:
-                        a_in(t + 2).start()
-
-                for i in range(2):
-                    when(t == parts - 2 + i, late[i].start)
+                    for which in range(2):
+
+                        @pl.when(t == which)
+                        def _():
+                            for c in late(which):
+                                c.start()
+
 
             r = rows(t, big)
             if deep:
@@ -479,9 +492,9 @@
                 for i in range(chunks):
                     flat_in(i).start()
 
-        when(j == 0, late[0].wait)
+        when(j == 0, lambda: [c.wait() for c in late(0)])
         td[slot] = dot(dytv[...], act[...]).T.astype(BF16)
-        when(j == 0, late[1].wait)
+        when(j == 0, lambda: [c.wait() for c in late(1)])
         if deep:
             both = dot(atv[...], dgu[...]).astype(BF16)
             tg[slot, 0] = both[:, :hidden]
@@ -509,8 +522,11 @@
         def ins(t):
             s = lax.rem(t, 2)
             return (
-                pltpu.make_async_copy(dgu_o.at[rows(t, tile)], wide.at[s], psem.at[s, 0]),
-                pltpu.make_async_copy(extra.at[rows(t, tile)], hst.at[s], psem.at[s, 1]),
+                *(
+                    pltpu.make_async_copy(dgu_o.at[rows(4 * t + i, tile // 4)], wide.at[s, rows(i, tile // 4)], psem.at[s, i])
+                    for i in range(4)
+                ),
+                pltpu.make_async_copy(extra.at[rows(t, tile)], hst.at[s], psem.at[s, 4]),
             )
 
         def outs(t):
@@ -610,14 +626,14 @@
         V((3, 2, dim, hidden), BF16), V((3, hidden, dim), BF16),
         V((chunks, 6, 2, own // 2, hidden), BF16), V((chunks, 6, share // 2, dim), BF16),
         V((8, hidden), F32), V((8, dim), F32),
-        DMA((chunks, 18)), DMA((chunks, 18)), DMA((3, tokens // big)), DMA((2, 2)),
+        DMA((chunks, 18)), DMA((chunks, 18)), DMA((4, max(n, tokens // big))), DMA((2, 2)),
     ]
     if deep:
         out_shape += [S((tokens, chunks * 2 * hidden), BF16), S((tokens, dim), BF16), S((dim, tokens), BF16)]
         out_specs += [ANY] * 3
         scratch += [
             V((2, dim, 2 * hidden), BF16), V((dim, chunks * 2 * hidden), BF16), V((2, tile, chunks * 2 * hidden), BF16), V((2, tile, dim), BF16),
-            V((2, dim, tile), BF16), DMA((1,)), DMA((chunks,)), DMA((2, 2)), DMA((2, 2)),
+            V((2, dim, tile), BF16), DMA((1,)), DMA((chunks,)), DMA((2, 5)), DMA((2, 2)),
         ]
     else:
         scratch += [V((n, 8, 128), F32), DMA((2, 3))]

time: 320 us -> 319 us (level)
  no operation moved by 1% of the time
where the time goes in v3:
time: 319 us
  Pallas kernels  318 us (100%)
    pallas_call x2, Pallas kernels, backward(): pl.pallas_call(functools.partial(backward_kernel, n, deep), out_shape=out...  218 us
    pallas_call x1, Pallas kernels, forward(): pl.pallas_call(functools.partial(forward_kernel, n), out_shape=[S((layers...  82.9 us
    pallas_call x1, Pallas kernels, update(): pl.pallas_call(functools.partial(update_kernel, n, count), grid=(layers,...  17.3 us

profile of v3, /device:TPU:112, one launch (start us, length us, event | category | flops | bytes accessed | tf_op | source)
XLA Modules:
  0.0 318.7 jit_solution(3148454542599909504)
XLA Ops:
  0.6 82.9 %forward.1 = (bf16[2,7,768,512]{3,2,1,0:T(8,128)(2,1)}, bf16[2,7,256,768]{3,2,1,0:T(8,128)(2,1)}, f32[7,4096,512]{2,1,0:T(8,128)}, bf16[768,4096]{1,0:T(8,128)(2...) custom-call(bf16[4096,768]{1,0:T(8,128)(2,1)} %bitcast.6, ...), custom_call_target="tpu_custom_call" | custom-call | tf_op jit(solution)/shard_map/forward/pallas_call | solution.py:299
  83.5 123.8 %backward_deep.1 = (bf16[7,192,512]{2,1,0:T(8,128)(2,1)}, bf16[7,64,768]{2,1,0:T(8,128)(2,1)}, f32[8,128]{1,0:T(8,128)}, bf16[4096,3584]{1,0:T(8,128)(2,1)}, bf1...) custom-call(bf16[4096,768]{1,0:T(8,128)(2,1)} %get-tuple-element.27.refs_0_, ...), custom_call_target="tpu_custom_call" | custom-call | tf_op jit(solution)/shard_map/backward_deep/pallas_call | solution.py:640
  207.3 94.0 %backward_first.1 = (bf16[7,192,512]{2,1,0:T(8,128)(2,1)}, bf16[7,64,768]{2,1,0:T(8,128)(2,1)}, f32[8,128]{1,0:T(8,128)}) custom-call(f32[7,4096,512]{2,1,0:T(8,128)} %get-tuple-element.25.refs_0_, bf16[768,4096]{1,0:T(8,128)(2,1)} %get-tuple-element.26.refs_1_, bf16[4096,768]{1,0:T(8,128)(2,1)} %get-tuple-element.33.refs_2_, ...), custom_call_target="tpu_custom_call" | custom-call | tf_op jit(solution)/shard_map/backward_first/pallas_call | solution.py:640
  301.3 17.3 %update.1 = (bf16[2,192,1792]{2,1,0:T(8,128)(2,1)}, bf16[2,192,1792]{2,1,0:T(8,128)(2,1)}, bf16[2,448,768]{2,1,0:T(8,128)(2,1)}, f32[2,192,1792]{2,1,0:T(8,128)}...) custom-call(f32[8,128]{1,0:T(8,128)} %get-tuple-element.36.sq, ...), custom_call_target="tpu_custom_call" | custom-call | tf_op jit(solution)/shard_map/update/pallas_call | solution.py:683
